TPU v7x, 32 devices: a whole 2x2x4 slice. The times are simulated.
32 devices in a mesh: member: 8 (over y, x, core), lat: 4 (over z).
Axes of the slice: x: 2, y: 2, z: 4, core: 2. Of those that a mesh axis runs over, the one named last changes fastest.
Arguments:
- ensemble: float32 [16, 3, 1, 32, 1440], P('member', None, None, 'lat'), may hold values from -6 to 6
- observation: float32 [3, 1, 32, 1440], P(None, None, 'lat'), may hold values from -6 to 6
- valid_mask: int32 [16], P('member'), may hold values from 0 to 1, as said below
- band_start: int32 [4], P('lat'), may hold values from 0 to 713
Outputs:
- crps_field: float32 [3, 1, 32, 1440], P(None, None, ('lat', 'member'))
- score_table: float32 [3, 1], replicated
Inputs may be any that keep to these rules, and one draw needn't show every extreme that they name: `valid_mask`: exactly 13 entries are 1, at positions drawn afresh.
All inputs are finite; a program needn't handle non-finite values.
Results may differ from a plain program's by a relative error of at most 0.0001.
Values sent between devices are 32-bit elements; how exact they have to be, the bound alone decides.
A program may use at most 64 MiB of HBM per device.

v0:
```python
import math
import jax
import jax.numpy as jnp
from jax import lax
from jax.sharding import PartitionSpec as P

GRID_LAT = 721
GRID_LON = 1440


def on_device(ensemble, observation, valid_mask, band_start):
    member_flags = valid_mask.astype(jnp.float32)
    lat_rows = ensemble.shape[3]
    block_rows = lat_rows // lax.axis_size("member")
    row_offset = lax.axis_index("member") * block_rows
    members = lax.all_to_all(ensemble, "member", split_axis=3, concat_axis=0, tiled=True)
    all_flags = lax.all_gather(member_flags, "member", axis=0, tiled=True)
    slot_total = members.shape[0]
    truth_slice = lax.dynamic_slice_in_dim(observation, row_offset, block_rows, 2)
    valid_count = jnp.sum(all_flags)
    flag_column = all_flags[:, None, None, None, None]
    skill_term = jnp.sum(flag_column * jnp.abs(members - truth_slice[None]), axis=0)
    group_count = slot_total // 8
    blocks = members.reshape((group_count, 8) + members.shape[1:])
    block_flags = all_flags.reshape(group_count, 8)

    def block_sum(block_item):
        block_slab, flags_here = block_item

        def add_one(position, running_sum):
            one_slab = lax.dynamic_index_in_dim(block_slab, position, 0, keepdims=True)
            one_flag = lax.dynamic_index_in_dim(flags_here, position, 0, keepdims=False)
            return running_sum + one_flag * jnp.sum(
                flag_column * jnp.abs(one_slab - members), axis=0
            )

        return lax.fori_loop(0, 8, add_one, jnp.zeros(truth_slice.shape, jnp.float32))

    spread = jnp.sum(lax.map(block_sum, (blocks, block_flags)), axis=0)
    crps_field = skill_term / valid_count - spread / (2.0 * valid_count * (valid_count - 1.0))
    row_index = (band_start[0] + row_offset + jnp.arange(block_rows, dtype=jnp.int32)).astype(
        jnp.float32
    )
    weight = jnp.cos((90.0 - row_index * 180.0 / (GRID_LAT - 1)) * math.pi / 180.0)
    partial_sums = jnp.sum(crps_field * weight[:, None], axis=(2, 3))
    totals = lax.psum(partial_sums, ("member", "lat"))
    score_table = totals / (lax.axis_size("lat") * lat_rows * GRID_LON)
    return (crps_field, score_table)


def solution(mesh):
    placed = (
        P("member", None, None, "lat", None),
        P(None, None, "lat", None),
        P("member"),
        P("lat"),
    )
    return jax.shard_map(
        on_device,
        mesh=mesh,
        in_specs=placed,
        out_specs=(P(None, None, ("lat", "member"), None), P()),
        check_vma=False,
    )
```

profile of v0, /device:TPU:0, one launch (start us, length us, event | category | flops | bytes accessed | tf_op | source)
XLA Modules:
  0.0 100.7 jit_solution(13239071511892019307)
XLA Ops:
  0.6 1.9 %copy.26 = f32[2,3,1,8,1440]{4,1,2,0,3:T(4,128)} copy(f32[2,3,1,8,1440]{4,3,2,1,0:T(8,128)} %param.8) | data formatting | bytes 552960 | tf_op args[0]
  2.6 5.2 %all-to-all-start = ((f32[2,3,1,8,1440]{4,1,2,0,3:T(4,128)}), f32[2,3,1,8,1440]{4,1,2,0,3:T(4,128)S(1)}, u32[]{:S(2)}, u32[]{:S(2)}) async-start(f32[2,3,1,8,1440]{4,1,2,0,3:T(4,128)} %copy.26), calls=%async_computation | async-start | bytes 786432 | tf_op jit(solution)/shard_map/all_to_all | solution.py:16
  7.8 0.6 copy-done.2
  8.4 0.6 dynamic-slice
  9.7 0.6 copy-done.1
  10.4 14.4 %all-reduce = f32[16]{0:T(128)S(1)} all-reduce(f32[16]{0:T(128)S(1)} %convert_dynamic-update-slice_fusion), channel_id=1, replica_groups=mesh['member'=8,'lat'=4] {'member'}, use_global_device_ids=true, to_apply=%add | all-reduce | flops 16 | bytes 128
  25.0 0.7 reduce_sum.50
  27.8 0.2 multiply_reduce_fusion.1
  28.0 0.3 copy.28
  28.3 31.1 %while.25 = (s32[]{:T(128)}, f32[2,3,1,1,1440]{4,3,2,1,0:T(1,128)S(1)}, f32[2,8,3,1,1,1440]{5,4,3,2,1,0:T(1,128)S(1)}, f32[2,8]{1,0:T(2,128)S(1)}, f32[16,1,1,1,...) while((s32[]{:T(128)}, ...), condition=%wide.region_6.7_spmd, body=%wide.region_2.6_spmd.sunk | while | flops 285125 | bytes 780332 | solution.py:39
  28.4 15.4 %while.26 = (s32[]{:T(128)}, f32[3,1,1,1440]{3,2,1,0:T(1,128)S(1)}, f32[8]{0:T(128)S(1)}, f32[16,1,1,1,1]{0,4,3,2,1:T(1,128)S(1)}, f32[8,3,1,1,1440]{4,3,2,1,0:T...) while((s32[]{:T(128)}, f32[3,1,1,1440]{3,2,1,0:T(1,128)S(1)}, ...), condition=%wide.region_5.5_spmd.clone, body=%wide.region_3.4_spmd.clone.sunk | while | flops 285123 | bytes 466739 | solution.py:37
  28.4 0.5 multiply_reduce_fusion.4
  28.9 0.7 dynamic_slice.43
  29.6 0.7 broadcast_multiply_fusion.3
  30.4 0.5 multiply_reduce_fusion.4
  30.8 0.7 dynamic_slice.43
  31.5 0.7 broadcast_multiply_fusion.3
  32.3 0.5 multiply_reduce_fusion.4
  32.8 0.7 dynamic_slice.43
  33.4 0.7 broadcast_multiply_fusion.3
  34.2 0.5 multiply_reduce_fusion.4
  34.7 0.7 dynamic_slice.43
  35.4 0.7 broadcast_multiply_fusion.3
  36.2 0.5 multiply_reduce_fusion.4
  36.6 0.7 dynamic_slice.43
  37.3 0.7 broadcast_multiply_fusion.3
  38.1 0.5 multiply_reduce_fusion.4
  38.6 0.7 dynamic_slice.43
  39.2 0.7 broadcast_multiply_fusion.3
  40.0 0.5 multiply_reduce_fusion.4
  40.5 0.7 dynamic_slice.43
  41.2 0.7 broadcast_multiply_fusion.3
  41.9 0.5 multiply_reduce_fusion.4
  42.4 0.7 dynamic_slice.43
  43.1 0.7 broadcast_multiply_fusion.3
  43.9 15.4 %while.26 = (s32[]{:T(128)}, f32[3,1,1,1440]{3,2,1,0:T(1,128)S(1)}, f32[8]{0:T(128)S(1)}, f32[16,1,1,1,1]{0,4,3,2,1:T(1,128)S(1)}, f32[8,3,1,1,1440]{4,3,2,1,0:T...) while((s32[]{:T(128)}, f32[3,1,1,1440]{3,2,1,0:T(1,128)S(1)}, ...), condition=%wide.region_5.5_spmd.clone, body=%wide.region_3.4_spmd.clone.sunk | while | flops 285123 | bytes 466739 | solution.py:37
  44.0 0.5 multiply_reduce_fusion.4
  44.4 0.7 dynamic_slice.43
  45.1 0.7 broadcast_multiply_fusion.3
  45.9 0.5 multiply_reduce_fusion.4
  46.4 0.7 dynamic_slice.43
  47.0 0.7 broadcast_multiply_fusion.3
  47.8 0.5 multiply_reduce_fusion.4
  48.3 0.7 dynamic_slice.43
  49.0 0.7 broadcast_multiply_fusion.3
  49.8 0.5 multiply_reduce_fusion.4
  50.2 0.7 dynamic_slice.43
  50.9 0.7 broadcast_multiply_fusion.3
  51.7 0.5 multiply_reduce_fusion.4
  52.2 0.7 dynamic_slice.43
  52.8 0.7 broadcast_multiply_fusion.3
  53.6 0.5 multiply_reduce_fusion.4
  54.1 0.7 dynamic_slice.43
  54.8 0.7 broadcast_multiply_fusion.3
  55.6 0.5 multiply_reduce_fusion.4
  56.0 0.7 dynamic_slice.43
  56.7 0.7 broadcast_multiply_fusion.3
  57.5 0.5 multiply_reduce_fusion.4
  57.9 0.7 dynamic_slice.43
  58.6 0.7 broadcast_multiply_fusion.3
  59.5 0.8 multiply_reduce_fusion.2
  60.2 0.6 sub.70
  60.8 39.4 %psum.7 = f32[3,1]{0,1:T(1,128)S(1)} all-reduce(f32[3,1]{0,1:T(1,128)S(1)} %bitcast.50), channel_id=1, replica_groups=mesh['member'=8,'lat'=4] {'member','lat'}, use_global_device_ids=true, to_apply=%region_9.10 | all-reduce | flops 3 | bytes 24 | tf_op jit(solution)/shard_map/psum | solution.py:46
  100.2 0.5 broadcast_multiply_fusion.1
  (70 shorter events, 1.6 us)
Async XLA Ops:
  0.6 25.0 %copy-start = (f32[3,1,8,1440]{3,2,1,0:T(8,128)S(1)}, f32[3,1,8,1440]{3,2,1,0:T(8,128)}, u32[]{:S(2)}) copy-start(f32[3,1,8,1440]{3,2,1,0:T(8,128)} %param.9) | copy-start | bytes 414724
  2.6 25.2 %all-to-all-start = ((f32[2,3,1,8,1440]{4,1,2,0,3:T(4,128)}), f32[2,3,1,8,1440]{4,1,2,0,3:T(4,128)S(1)}, u32[]{:S(2)}, u32[]{:S(2)}) async-start(f32[2,3,1,8,1440]{4,1,2,0,3:T(4,128)} %copy.26), calls=%async_computation | async-start | bytes 786432 | tf_op jit(solution)/shard_map/all_to_all | solution.py:16
  7.8 0.7 copy-start.2
  9.7 0.7 copy-start.1
where the time goes:
time: 101 us
  blocking collectives  53.8 us (53%)
  other arithmetic  21.6 us (21%)
  local copies, waits for them, and re-layouts  16.1 us (16%)
  starting transfers between devices  5.2 us (5%)
  between operations  3.34 us (3%)
    psum x1, blocking collectives, on_device(): totals = lax.psum(partial_sums, ('member', 'lat'))  39.4 us
    unnamed x1, blocking collectives  14.4 us
    mul x16, other arithmetic, add_one(): one_flag * jnp.sum(flag_column * jnp.abs(one_slab - members), axis=0)  11.1 us
    dynamic_slice x16, local copies, waits for them, and re-layouts, add_one(): one_flag = lax.dynamic_index_in_dim(flags_here, position, 0, keepdims=False)  10.7 us
    reduce_sum x16, other arithmetic, add_one(): jnp.sum(flag_column * jnp.abs(one_slab - members), axis=0)  7.4 us
    all_to_all x1, starting transfers between devices, on_device(): lax.all_to_all(ensemble, 'member', split_axis=3, concat_axis=0, tiled=True)  5.2 us
    unnamed x10, local copies, waits for them, and re-layouts  3.83 us
  transfers between devices with their start and end apart: 1, of which 0 were waited for; matrix products, arithmetic and copies ran while one was open for 2% of the time, Pallas kernels for 0%

commit v1 on v0

--- a/solution.py
+++ b/solution.py
@@ -13,7 +13,12 @@
     lat_rows = ensemble.shape[3]
     block_rows = lat_rows // lax.axis_size("member")
     row_offset = lax.axis_index("member") * block_rows
-    members = lax.all_to_all(ensemble, "member", split_axis=3, concat_axis=0, tiled=True)
+    members = jnp.concatenate(
+        lax.all_to_all(
+            jnp.stack(jnp.split(ensemble, lax.axis_size("member"), axis=3)), "member", 0, 0
+        ),
+        axis=0,
+    )
     all_flags = lax.all_gather(member_flags, "member", axis=0, tiled=True)
     slot_total = members.shape[0]
     truth_slice = lax.dynamic_slice_in_dim(observation, row_offset, block_rows, 2)

time: 101 us -> 112 us (1.11)
  local copies, waits for them, and re-layouts: 16.1 us -> 26.6 us
    unnamed x10 -> x16, local copies, waits for them, and re-layouts: 3.83 us -> 13.1 us
    another operation x0 -> x1, local copies, waits for them, and re-layouts: none -> 1.6 us  [on_device(): jnp.stack(jnp.split(ensemble, lax.axis_size('member'), axis=3))]
  transfers between devices with their start and end apart: 1 -> 1, of which waited for: 0 -> 0; matrix products, arithmetic and copies ran while one was open for 2% -> 1% of each run, Pallas kernels for 0% -> 0%
where the time goes in v1:
time: 112 us; the launch traced here: 111 us
  blocking collectives  53.8 us (48%)
  local copies, waits for them, and re-layouts  26.6 us (24%)
  other arithmetic  21.6 us (19%)
  starting transfers between devices  5.2 us (5%)
  between operations  3.18 us (3%)
    psum x1, blocking collectives, on_device(): totals = lax.psum(partial_sums, ('member', 'lat'))  39.4 us
    unnamed x1, blocking collectives  14.4 us
    unnamed x16, local copies, waits for them, and re-layouts  13.1 us
    mul x16, other arithmetic, add_one(): one_flag * jnp.sum(flag_column * jnp.abs(one_slab - members), axis=0)  11.1 us
    dynamic_slice x16, local copies, waits for them, and re-layouts, add_one(): one_flag = lax.dynamic_index_in_dim(flags_here, position, 0, keepdims=False)  10.7 us
    reduce_sum x16, other arithmetic, add_one(): jnp.sum(flag_column * jnp.abs(one_slab - members), axis=0)  7.4 us
    all_to_all x1, starting transfers between devices, on_device(): lax.all_to_all(jnp.stack(jnp.split(ensemble, lax.axis_size('member'), axi...  5.2 us
  transfers between devices with their start and end apart: 1, of which 0 were waited for; matrix products, arithmetic and copies ran while one was open for 1% of the time, Pallas kernels for 0%

profile of v1, /device:TPU:0, one launch (start us, length us, event | category | flops | bytes accessed | tf_op | source)
XLA Modules:
  0.0 111.2 jit_solution(15184062010731343617)
XLA Ops:
  0.6 1.6 %bitcast_dynamic-update-slice_fusion.8 = f32[8,2,3,1,1,1440]{5,4,3,2,1,0:T(1,128)} fusion(f32[2,3,1,8,1440]{4,3,2,1,0:T(8,128)} %param.8), kind=kLoop, calls=%fused_computation.18 | loop fusion | bytes 71424
  2.3 1.6 %bitcast_dynamic-update-slice_fusion.7 = f32[8,2,3,1,1,1440]{5,4,3,2,1,0:T(1,128)} fusion(f32[8,2,3,1,1,1440]{5,4,3,2,1,0:T(1,128)} %bitcast_dynamic-update-slice_fusion.8, f32[2,3,1,8,1440]{4,3,2,1,0:T(8,128)} %param.8), kind=kLoop, calls=%fused_computation.17 | loop fusion | bytes 73728
  3.9 1.6 %bitcast_dynamic-update-slice_fusion.6 = f32[8,2,3,1,1,1440]{5,4,3,2,1,0:T(1,128)} fusion(f32[8,2,3,1,1,1440]{5,4,3,2,1,0:T(1,128)} %bitcast_dynamic-update-slice_fusion.7, f32[2,3,1,8,1440]{4,3,2,1,0:T(8,128)} %param.8), kind=kLoop, calls=%fused_computation.16 | loop fusion | bytes 73728
  5.5 1.6 %bitcast_dynamic-update-slice_fusion.5 = f32[8,2,3,1,1,1440]{5,4,3,2,1,0:T(1,128)} fusion(f32[8,2,3,1,1,1440]{5,4,3,2,1,0:T(1,128)} %bitcast_dynamic-update-slice_fusion.6, f32[2,3,1,8,1440]{4,3,2,1,0:T(8,128)} %param.8), kind=kLoop, calls=%fused_computation.15 | loop fusion | bytes 73728
  7.1 1.6 %bitcast_dynamic-update-slice_fusion.4 = f32[8,2,3,1,1,1440]{5,4,3,2,1,0:T(1,128)} fusion(f32[8,2,3,1,1,1440]{5,4,3,2,1,0:T(1,128)} %bitcast_dynamic-update-slice_fusion.5, f32[2,3,1,8,1440]{4,3,2,1,0:T(8,128)} %param.8), kind=kLoop, calls=%fused_computation.14 | loop fusion | bytes 73728
  8.7 1.6 %bitcast_dynamic-update-slice_fusion.3 = f32[8,2,3,1,1,1440]{5,4,3,2,1,0:T(1,128)} fusion(f32[8,2,3,1,1,1440]{5,4,3,2,1,0:T(1,128)} %bitcast_dynamic-update-slice_fusion.4, f32[2,3,1,8,1440]{4,3,2,1,0:T(8,128)} %param.8), kind=kLoop, calls=%fused_computation.13 | loop fusion | bytes 73728
  10.3 1.6 %bitcast_dynamic-update-slice_fusion.2 = f32[8,2,3,1,1,1440]{5,4,3,2,1,0:T(1,128)} fusion(f32[8,2,3,1,1,1440]{5,4,3,2,1,0:T(1,128)} %bitcast_dynamic-update-slice_fusion.3, f32[2,3,1,8,1440]{4,3,2,1,0:T(8,128)} %param.8), kind=kLoop, calls=%fused_computation.12 | loop fusion | bytes 73728
  11.9 1.6 %bitcast_dynamic-update-slice_fusion.1 = f32[8,2,3,1,1,1440]{5,4,3,2,1,0:T(1,128)} fusion(f32[8,2,3,1,1,1440]{5,4,3,2,1,0:T(1,128)} %bitcast_dynamic-update-slice_fusion.2, f32[2,3,1,8,1440]{4,3,2,1,0:T(8,128)} %param.8), kind=kLoop, calls=%fused_computation.11 | loop fusion | bytes 73728 | tf_op jit(solution)/shard_map/stack | solution.py:18
  13.5 5.2 %all-to-all-start = ((f32[8,2,3,1,1,1440]{5,4,3,2,1,0:T(1,128)}), f32[8,2,3,1,1,1440]{5,4,3,2,1,0:T(1,128)S(1)}, u32[]{:S(2)}, u32[]{:S(2)}) async-start(f32[8,2,3,1,1,1440]{5,4,3,2,1,0:T(1,128)} %bitcast_dynamic-update-slice_fusion.1), calls=%async_computation | async-start | bytes 589824 | tf_op jit(solution)/shard_map/all_to_all | solution.py:17
  18.7 0.6 copy-done.2
  19.3 0.6 dynamic-slice
  20.6 0.6 copy-done.1
  21.3 14.4 %all-reduce = f32[16]{0:T(128)S(1)} all-reduce(f32[16]{0:T(128)S(1)} %convert_dynamic-update-slice_fusion), channel_id=1, replica_groups=mesh['member'=8,'lat'=4] {'member'}, use_global_device_ids=true, to_apply=%add | all-reduce | flops 16 | bytes 128
  35.9 0.6 reduce_sum.50
  38.3 31.1 %while.25 = (s32[]{:T(128)}, f32[2,3,1,1,1440]{4,3,2,1,0:T(1,128)S(1)}, f32[2,8,3,1,1,1440]{5,4,3,2,1,0:T(1,128)S(1)}, f32[2,8]{1,0:T(2,128)S(1)}, f32[16,1,1,1,...) while((s32[]{:T(128)}, ...), condition=%wide.region_6.7_spmd, body=%wide.region_2.6_spmd.sunk | while | flops 285125 | bytes 780332 | solution.py:44
  38.4 15.4 %while.26 = (s32[]{:T(128)}, f32[3,1,1,1440]{3,2,1,0:T(1,128)S(1)}, f32[8]{0:T(128)S(1)}, f32[16,1,1,1,1]{0,4,3,2,1:T(1,128)S(1)}, f32[8,3,1,1,1440]{4,3,2,1,0:T...) while((s32[]{:T(128)}, f32[3,1,1,1440]{3,2,1,0:T(1,128)S(1)}, ...), condition=%wide.region_5.5_spmd.clone, body=%wide.region_3.4_spmd.clone.sunk | while | flops 285123 | bytes 466739 | solution.py:42
  38.5 0.5 multiply_reduce_fusion.4
  38.9 0.7 dynamic_slice.43
  39.6 0.7 broadcast_multiply_fusion.3
  40.4 0.5 multiply_reduce_fusion.4
  40.9 0.7 dynamic_slice.43
  41.5 0.7 broadcast_multiply_fusion.3
  42.8 0.7 dynamic_slice.43
  43.5 0.7 broadcast_multiply_fusion.3
  44.7 0.7 dynamic_slice.43
  45.4 0.7 broadcast_multiply_fusion.3
  46.2 0.5 multiply_reduce_fusion.4
  46.6 0.7 dynamic_slice.43
  47.3 0.7 broadcast_multiply_fusion.3
  48.1 0.5 multiply_reduce_fusion.4
  48.6 0.7 dynamic_slice.43
  49.2 0.7 broadcast_multiply_fusion.3
  50.5 0.7 dynamic_slice.43
  51.2 0.7 broadcast_multiply_fusion.3
  52.0 0.5 multiply_reduce_fusion.4
  52.4 0.7 dynamic_slice.43
  53.1 0.7 broadcast_multiply_fusion.3
  53.9 15.4 %while.26 = (s32[]{:T(128)}, f32[3,1,1,1440]{3,2,1,0:T(1,128)S(1)}, f32[8]{0:T(128)S(1)}, f32[16,1,1,1,1]{0,4,3,2,1:T(1,128)S(1)}, f32[8,3,1,1,1440]{4,3,2,1,0:T...) while((s32[]{:T(128)}, f32[3,1,1,1440]{3,2,1,0:T(1,128)S(1)}, ...), condition=%wide.region_5.5_spmd.clone, body=%wide.region_3.4_spmd.clone.sunk | while | flops 285123 | bytes 466739 | solution.py:42
  54.0 0.5 multiply_reduce_fusion.4
  54.5 0.7 dynamic_slice.43
  55.1 0.7 broadcast_multiply_fusion.3
  55.9 0.5 multiply_reduce_fusion.4
  56.4 0.7 dynamic_slice.43
  57.1 0.7 broadcast_multiply_fusion.3
  58.3 0.7 dynamic_slice.43
  59.0 0.7 broadcast_multiply_fusion.3
  59.8 0.5 multiply_reduce_fusion.4
  60.2 0.7 dynamic_slice.43
  60.9 0.7 broadcast_multiply_fusion.3
  61.7 0.5 multiply_reduce_fusion.4
  62.2 0.7 dynamic_slice.43
  62.8 0.7 broadcast_multiply_fusion.3
  64.1 0.7 dynamic_slice.43
  64.8 0.7 broadcast_multiply_fusion.3
  66.0 0.7 dynamic_slice.43
  66.7 0.7 broadcast_multiply_fusion.3
  67.5 0.5 multiply_reduce_fusion.4
  68.0 0.7 dynamic_slice.43
  68.6 0.7 broadcast_multiply_fusion.3
  69.5 0.5 multiply_reduce_fusion.1
  70.0 0.7 multiply_reduce_fusion.2
  70.6 0.6 sub.70
  71.3 39.4 %psum.7 = f32[3,1]{0,1:T(1,128)S(1)} all-reduce(f32[3,1]{0,1:T(1,128)S(1)} %bitcast.58), channel_id=1, replica_groups=mesh['member'=8,'lat'=4] {'member','lat'}, use_global_device_ids=true, to_apply=%region_9.10 | all-reduce | flops 3 | bytes 24 | tf_op jit(solution)/shard_map/psum | solution.py:51
  110.6 0.5 broadcast_multiply_fusion.1
  (75 shorter events, 4.3 us)
Async XLA Ops:
  0.6 35.8 %copy-start = (f32[3,1,8,1440]{3,2,1,0:T(8,128)S(1)}, f32[3,1,8,1440]{3,2,1,0:T(8,128)}, u32[]{:S(2)}) copy-start(f32[3,1,8,1440]{3,2,1,0:T(8,128)} %param.9) | copy-start | bytes 414724
  13.5 24.8 %all-to-all-start = ((f32[8,2,3,1,1,1440]{5,4,3,2,1,0:T(1,128)}), f32[8,2,3,1,1,1440]{5,4,3,2,1,0:T(1,128)S(1)}, u32[]{:S(2)}, u32[]{:S(2)}) async-start(f32[8,2,3,1,1,1440]{5,4,3,2,1,0:T(1,128)} %bitcast_dynamic-update-slice_fusion.1), calls=%async_computation | async-start | bytes 589824 | tf_op jit(solution)/shard_map/all_to_all | solution.py:17
  18.7 0.7 copy-start.2
  20.6 0.7 copy-start.1
